TPU v7x, 16 devices: a whole 2x2x2 slice. The times are simulated.
16 devices in a mesh: stage: 2 (over z), expert: 8 (over y, x, core).
Axes of the slice: x: 2, y: 2, z: 2, core: 2. Of those that a mesh axis runs over, the one named last changes fastest.
Arguments:
- w_gate: bfloat16 [4, 8, 2048, 1024], P('stage', 'expert')
- w_up: bfloat16 [4, 8, 2048, 1024], P('stage', 'expert')
- w_down: bfloat16 [4, 8, 1024, 2048], P('stage', 'expert')
- dense: bfloat16 [4, 2048, 2048], P('stage')
- hot_ids: int32 [2], replicated
- spare_map: int32 [16], P(('stage', 'expert'))
Outputs:
- output 1: bfloat16 [4, 16, 2048, 1024], P(None, ('stage', 'expert'))
- output 2: bfloat16 [4, 16, 512, 2048], P(None, ('stage', 'expert'))
- output 3: bfloat16 [4, 2048, 2048], replicated
- output 4: bfloat16 [4, 16, 2048, 1024], P(None, ('stage', 'expert'))
- output 5: bfloat16 [4, 16, 512, 2048], P(None, ('stage', 'expert'))
All inputs are finite; a program needn't handle non-finite values.
Results may differ from a plain program's by a relative error of at most 0.001.
Values are sent between devices in bfloat16 or wider.
A program may use at most 1 GiB of HBM per device.

v0:
```python
import jax
import jax.numpy as jnp
from jax import lax
from jax.sharding import PartitionSpec as P


def solution(mesh):
    stage_count = mesh.shape['stage']
    group_count = mesh.shape['expert']
    device_count = stage_count * group_count
    flat_axes = ('stage', 'expert')
    pair_list = [(pos * group_count + col, col * stage_count + pos) for pos in range(stage_count) for col in range(group_count)]

    def local_move(w_gate, w_up, w_down, dense, hot_ids, spare_map):
        layer_local, expert_local, d_model, ff_width = w_gate.shape
        expert_total = expert_local * group_count
        pieces = max(1, device_count // expert_total)
        piece_width = ff_width // pieces
        unit_local = expert_local * pieces
        gate_parts = w_gate.reshape(layer_local, expert_local, d_model, pieces, piece_width)
        up_parts = w_up.reshape(layer_local, expert_local, d_model, pieces, piece_width)
        gate_up = jnp.concatenate([gate_parts, up_parts], axis=-1)
        gate_up = jnp.transpose(gate_up, (0, 1, 3, 2, 4)).reshape(layer_local, unit_local, d_model, 2 * piece_width)
        down_units = w_down.reshape(layer_local, unit_local, piece_width, d_model)

        local_ids = lax.axis_index('expert') * unit_local + jnp.arange(unit_local)
        owned_mask = (hot_ids[:, None] == local_ids[None, :]).astype(jnp.bfloat16)
        hot_gate_up = jnp.einsum('hu,ludf->lhdf', owned_mask, gate_up, preferred_element_type=jnp.float32).astype(jnp.bfloat16)
        hot_down = jnp.einsum('hu,lufd->lhfd', owned_mask, down_units, preferred_element_type=jnp.float32).astype(jnp.bfloat16)
        hot_gate_up = lax.psum(hot_gate_up, 'expert')
        hot_down = lax.psum(hot_down, 'expert')
        hot_gate_up = lax.all_gather(hot_gate_up, 'stage', axis=0, tiled=True)
        hot_down = lax.all_gather(hot_down, 'stage', axis=0, tiled=True)
        slot_pick = (spare_map[:, None] == jnp.arange(hot_ids.shape[0])[None, :]).astype(jnp.bfloat16)
        spare_gate_up = jnp.einsum('nh,lhdf->lndf', slot_pick, hot_gate_up, preferred_element_type=jnp.float32).astype(jnp.bfloat16)
        spare_down = jnp.einsum('nh,lhfd->lnfd', slot_pick, hot_down, preferred_element_type=jnp.float32).astype(jnp.bfloat16)

        gate_up = lax.all_to_all(gate_up, 'stage', 1, 0, tiled=True)
        down_units = lax.all_to_all(down_units, 'stage', 1, 0, tiled=True)
        gate_up = lax.ppermute(gate_up, flat_axes, pair_list)
        down_units = lax.ppermute(down_units, flat_axes, pair_list)
        dense_all = lax.all_gather(dense, 'stage', axis=0, tiled=True)
        return gate_up, down_units, dense_all, spare_gate_up, spare_down

    expert_spec = P('stage', 'expert', None, None)
    unit_spec = P(None, flat_axes, None, None)
    return jax.shard_map(
        local_move,
        mesh=mesh,
        in_specs=(expert_spec, expert_spec, expert_spec, P('stage', None, None), P(None), P(flat_axes)),
        out_specs=(unit_spec, unit_spec, P(None, None, None), unit_spec, unit_spec),
        check_vma=False,
    )
```

profile of v0, /device:TPU:0, one launch (start us, length us, event | category | flops | bytes accessed | tf_op | source)
XLA Modules:
  0.0 2231.9 jit_solution(15076059709187447214)
XLA Ops:
  7.2 14.5 reshape.42
  21.7 8.2 copy.14
  29.9 14.4 reshape.43
  44.3 8.2 copy.15
  52.5 8.4 maximum_bitcast_fusion
  60.9 83.0 %fusion.4 = bf16[2,2048,1024,2]{2,3,1,0:T(2,128)(2,1)} fusion(bf16[2,2,2048,1024]{3,2,0,1:T(8,128)(2,1)S(1)} %maximum_bitcast_fusion, s32[2]{0:T(128)S(1)} %iota_add_fusion, s32[2]{0:T(128)S(1)} %copy-done.1), kind=kOutput, calls=%fused_computation.9 | convolution fusion | flops 33554436 | bytes 33554448 | tf_op jit(solution)/shard_map/hu,ludf->lhdf/dot_general | solution.py:28
  143.9 16.5 copy.51
  160.4 31.7 %fusion.10 = bf16[2,2,512,2048]{3,0,2,1:T(2,128)(2,1)} fusion(bf16[2,2,512,2048]{3,2,1,0:T(8,128)(2,1)} %bitcast.68, s32[2]{0:T(128)S(1)} %iota_add_fusion, s32[2]{0:T(128)S(1)} %copy-done.1), kind=kOutput, calls=%fused_computation.15 | convolution fusion | flops 16777220 | bytes 16777232 | tf_op jit(solution)/shard_map/hu,lufd->lhfd/dot_general | solution.py:29
  192.1 10.7 copy.53
  202.8 301.8 %all-reduce.3.cloned.1.call-done = (bf16[2,2,2048,1024]{3,2,1,0:T(8,128)(2,1)}, bf16[2,2,512,2048]{3,2,0,1:T(8,128)(2,1)}) async-done(((bf16[2,2,2048,1024]{3,2,1,0:T(8,128)(2,1)}, bf16[2,2,512,2048]{3,2,0,1:T(8,128)(2,1)}), (bf16[2,2,2048,1024]{3,2,1,0:T(8,128)(2,1)}, bf16[2,2,512,2048]{3,2,0,1:T(8,128)(2,1)})) %all-reduce.3.cloned.1.call-update) | async-done | bytes 25165840 | tf_op jit(solution)/shard_map/psum | solution.py:30
  504.7 0.7 all-gather.4.cloned.1.call-update
  506.0 377.6 %all_to_all.36 = bf16[2,2,2048,1024]{3,2,0,1:T(8,128)(2,1)} all-to-all(bf16[2,2,2048,1024]{3,2,0,1:T(8,128)(2,1)} %copy-done), channel_id=1, replica_groups=mesh['stage'=2,'expert'=8] {'stage'}, dimensions={1} | all-to-all | bytes 33554432 | tf_op jit(solution)/shard_map/all_to_all | solution.py:38
  883.5 126.7 %collective-permute-start = (bf16[4,1,2048,1024]{3,2,1,0:T(8,128)(2,1)}, bf16[4,1,2048,1024]{3,2,1,0:T(8,128)(2,1)}, u32[]{:S(2)}, u32[]{:S(2)}) collective-permute-start(bf16[4,1,2048,1024]{3,2,1,0:T(8,128)(2,1)} %bitcast.4), channel_id=1, source_target_pairs={{0,0},{1,2},{2,4},{3,6},{4,8},{5,10},{6,12},{7,14},{8,1},{9,3},{10... | collective-permute-start | bytes 50331656 | tf_op jit(solution)/shard_map/ppermute | solution.py:40
  1010.2 8.4 copy.16
  1018.6 498.9 %all_to_all.37 = bf16[2,2,512,2048]{3,2,0,1:T(8,128)(2,1)S(1)} all-to-all(bf16[2,2,512,2048]{3,2,0,1:T(8,128)(2,1)} %copy.16), channel_id=1, replica_groups=mesh['stage'=2,'expert'=8] {'stage'}, dimensions={1} | all-to-all | bytes 16777216 | tf_op jit(solution)/shard_map/all_to_all | solution.py:39
  1517.5 3.9 collective-permute-start.1
  1522.1 29.1 %fusion.6 = bf16[1,4,512,2048]{3,0,2,1:T(2,128)(2,1)S(1)} fusion(bf16[4,2,512,2048]{3,2,0,1:T(8,128)(2,1)} %all-gather.8.cloned.1.call-done, s32[]{:T(128)} %bitcast.63), kind=kOutput, calls=%fused_computation.11 | convolution fusion | flops 16777218 | bytes 25165828 | tf_op jit(solution)/shard_map/nh,lhfd->lnfd/dot_general | solution.py:36
  1551.2 6.6 copy.54
  1557.8 438.5 %all-gather.6.cloned.1.call-done = bf16[4,2,2048,1024]{3,2,1,0:T(8,128)(2,1)} async-done(((bf16[2,2,2048,1024]{3,2,1,0:T(8,128)(2,1)}), bf16[4,2,2048,1024]{3,2,1,0:T(8,128)(2,1)}) %all-gather.6.cloned.1.call-update) | async-done | bytes 33554448 | tf_op jit(solution)/shard_map/all_gather | solution.py:32
  1996.3 161.2 %fusion = bf16[1,4,2048,1024]{3,0,2,1:T(2,128)(2,1)} fusion(bf16[4,2,2048,1024]{3,2,1,0:T(8,128)(2,1)} %all-gather.6.cloned.1.call-done, s32[]{:T(128)} %bitcast.62), kind=kOutput, calls=%fused_computation.2 | convolution fusion | flops 33554432 | bytes 50331652 | tf_op jit(solution)/shard_map/nh,lhdf->lndf/dot_general | solution.py:35
  2157.5 22.2 copy.52
  2179.7 13.9 copy.61
  2193.6 8.4 copy.62
  2202.0 22.9 %copy.63 = bf16[4,2048,2048]{2,1,0:T(8,128)(2,1)} copy(bf16[4,2048,2048]{2,1,0:T(8,128)(2,1)} %all-gather.4.cloned.1.call-done) | data formatting | bytes 67108864
  (16 shorter events, 0.8 us)
Async XLA Ops:
  7.2 497.5 %all-reduce.3.cloned.1.call-start = ((), (), s32[]{:S(2)}) async-start(), calls=%async_computation.5 | async-start | bytes 50331648 | tf_op jit(solution)/shard_map/psum | solution.py:30
  52.5 8.4 copy-start.1
  60.9 83.0 %copy-start = (bf16[2,2,2048,1024]{3,2,0,1:T(8,128)(2,1)}, bf16[2,2,2048,1024]{3,2,0,1:T(8,128)(2,1)S(1)}, u32[]{:S(2)}) copy-start(bf16[2,2,2048,1024]{3,2,0,1:T(8,128)(2,1)S(1)} %maximum_bitcast_fusion) | copy-start | bytes 50331652
  202.8 1319.3 %all-gather.8.cloned.1.call-start = ((), (), s32[]{:S(2)}) async-start(), calls=%async_computation.4 | async-start | bytes 25165824 | tf_op jit(solution)/shard_map/all_gather | solution.py:33
  504.7 1053.2 %all-gather.4.cloned.1.call-start = ((), (), s32[]{:S(2)}) async-start(), calls=%async_computation.2 | async-start | bytes 50331648 | tf_op jit(solution)/shard_map/all_gather | solution.py:42
  505.4 1490.9 %all-gather.6.cloned.1.call-start = ((), (), s32[]{:S(2)}) async-start(), calls=%async_computation.3 | async-start | bytes 50331648 | tf_op jit(solution)/shard_map/all_gather | solution.py:32
  883.5 638.5 %collective-permute-start = (bf16[4,1,2048,1024]{3,2,1,0:T(8,128)(2,1)}, bf16[4,1,2048,1024]{3,2,1,0:T(8,128)(2,1)}, u32[]{:S(2)}, u32[]{:S(2)}) collective-permute-start(bf16[4,1,2048,1024]{3,2,1,0:T(8,128)(2,1)} %bitcast.4), channel_id=1, source_target_pairs={{0,0},{1,2},{2,4},{3,6},{4,8},{5,10},{6,12},{7,14},{8,1},{9,3},{10... | collective-permute-start | bytes 50331656 | tf_op jit(solution)/shard_map/ppermute | solution.py:40
  1517.5 4.5 collective-permute-start.1
Sparse Core Ops, SparseCore 0:
  202.9 301.6 all-reduce.2
  506.2 375.2 all-gather.7
  883.0 633.8 all-gather.3
  1518.3 477.9 all-gather.5
where the time goes:
time: 2250 us; the launch traced here: 2230 us
  blocking collectives  876 us (39%)
  waiting for transfers between devices  742 us (33%)
  matrix products  305 us (14%)
  local copies, waits for them, and re-layouts  155 us (7%)
  starting transfers between devices  131 us (6%)
    all_to_all x1, blocking collectives, local_move(): down_units = lax.all_to_all(down_units, 'stage', 1, 0, tiled=True)  499 us
    all_gather x1, waiting for transfers between devices, local_move(): hot_gate_up = lax.all_gather(hot_gate_up, 'stage', axis=0, tiled=True)  439 us
    all_to_all x1, blocking collectives, local_move(): gate_up = lax.all_to_all(gate_up, 'stage', 1, 0, tiled=True)  378 us
    psum x1, waiting for transfers between devices, local_move(): hot_gate_up = lax.psum(hot_gate_up, 'expert')  302 us
    dot_general x1, matrix products, local_move(): jnp.einsum('nh,lhdf->lndf', slot_pick, hot_gate_up, preferred_element_typ...  161 us
    ppermute x1, starting transfers between devices, local_move(): gate_up = lax.ppermute(gate_up, flat_axes, pair_list)  127 us
    dot_general x1, matrix products, local_move(): jnp.einsum('hu,ludf->lhdf', owned_mask, gate_up, preferred_element_type=j...  83 us
    unnamed x7, local copies, waits for them, and re-layouts  45.2 us
  transfers between devices with their start and end apart: 6, of which 2 were waited for; matrix products, arithmetic and copies ran while one was open for 2% of the time, Pallas kernels for 0%

commit v1 on v0

v1 whole, which is shorter than its diff:
```python
import jax
import jax.numpy as jnp
from jax import lax
from jax.experimental import pallas as pl
from jax.experimental.pallas import tpu as pltpu
from jax.sharding import PartitionSpec as P

MESH = pl.DeviceIdType.MESH
ANY = pl.BlockSpec(memory_space=pl.ANY)
BF16 = jnp.bfloat16
DIRECT = 256
QUARTER = (2048 - DIRECT) // 4
HALF = QUARTER // 2
CHUNKS = 32


def coords():
    s = lax.axis_index('stage')
    g = lax.axis_index('expert')
    return s, g // 4, (g // 2) % 2, g % 2


def dev(z, y, x, c):
    return (z, y * 4 + x * 2 + c)


def remote(src, dst, send_sem, recv_sem, target):
    return pltpu.make_async_remote_copy(
        src_ref=src, dst_ref=dst, send_sem=send_sem, recv_sem=recv_sem,
        device_id=dev(*target), device_id_type=MESH)


def move_kernel(gate, up, down, dense, w13, w2, other, us, ur, ul, ds, dr):
    z, y, x, c = coords()
    is_s = c == x
    is_r = c != x

    def quarter(yy, xx):
        return pl.multiple_of(DIRECT + (yy * 2 + xx) * QUARTER, 32)

    q0 = quarter(y, x)
    zn = (1 - z, y, x, c)
    sib = (z, y, x, 1 - c)
    xn = (z, y, 1 - x, c)
    yn = (z, 1 - y, x, c)
    zq = remote(dense.at[c, pl.ds(q0, QUARTER)], other.at[c, pl.ds(q0, QUARTER)], ds.at[0], dr.at[0], zn)
    zd = remote(dense.at[c, pl.ds(0, DIRECT)], other.at[c, pl.ds(0, DIRECT)], ds.at[1], dr.at[1], zn)
    zq.start()
    zd.start()

    unit_copies = []
    for p in range(2):
        same = (y == z) & (x == y) & (c == x) & (p == c)
        dst_chip = (y, x, c, p)
        triples = [
            (gate.at[:, 0, :, pl.ds(p * 512, 512)], w13.at[pl.ds(2 * z, 2), 0, :, pl.ds(0, 512)]),
            (up.at[:, 0, :, pl.ds(p * 512, 512)], w13.at[pl.ds(2 * z, 2), 0, :, pl.ds(512, 512)]),
            (down.at[:, 0, pl.ds(p * 512, 512), :], w2.at[pl.ds(2 * z, 2), 0]),
        ]
        for k, (src, dst) in enumerate(triples):
            cp = remote(src, dst, us.at[p, k], ur.at[z, k], dst_chip)
            lc = pltpu.make_async_copy(src, dst, ul.at[k])
            unit_copies.append((same, cp, lc))
    for same, cp, lc in unit_copies:
        @pl.when(jnp.logical_not(same))
        def _():
            cp.start()

        @pl.when(same)
        def _():
            lc.start()

    def band(ref, start, size, layer=None):
        if layer is None:
            return ref.at[:, pl.ds(start, size)]
        return ref.at[layer, pl.ds(start, size)]

    zq.wait_recv()
    dq = remote(band(other, q0, QUARTER, c), band(other, q0, QUARTER, c), ds.at[2], dr.at[2], sib)
    dq.start()
    zd.wait_recv()
    dd = remote(band(other, 0, DIRECT, c), band(other, 0, DIRECT, c), ds.at[3], dr.at[3], sib)
    dd.start()
    dq.wait_recv()

    qx, qy, qd = quarter(y, 1 - x), quarter(1 - y, x), quarter(1 - y, 1 - x)
    xq = remote(band(other, q0, QUARTER), band(other, q0, QUARTER), ds.at[4], dr.at[4], xn)
    yq = remote(band(other, q0, QUARTER), band(other, q0, QUARTER), ds.at[5], dr.at[5], yn)
    ya = remote(band(other, qx, HALF), band(other, qx, HALF), ds.at[6], dr.at[6], yn)
    b0 = pl.multiple_of(qy + HALF, 32)
    xb = remote(band(other, b0, HALF), band(other, b0, HALF), ds.at[7], dr.at[7], xn)
    dx = remote(band(other, qx, QUARTER), band(other, qx, QUARTER), ds.at[8], dr.at[8], sib)
    dy = remote(band(other, qy, QUARTER), band(other, qy, QUARTER), ds.at[9], dr.at[9], sib)
    da = remote(band(other, qd, HALF), band(other, qd, HALF), ds.at[10], dr.at[10], sib)
    e0 = pl.multiple_of(qd + HALF, 32)
    db = remote(band(other, e0, HALF), band(other, e0, HALF), ds.at[11], dr.at[11], sib)

    @pl.when(is_s)
    def _():
        xq.start()
        dy.wait_recv()
        xb.start()
        dx.wait_recv()
        da.wait_recv()
        db.wait_recv()
        xq.wait_send()
        xb.wait_send()

    @pl.when(is_r)
    def _():
        yq.start()
        yq.wait_recv()
        dy.start()
        xq.wait_recv()
        ya.start()
        dx.start()
        ya.wait_recv()
        da.start()
        xb.wait_recv()
        db.start()
        for cp in (yq, ya, dx, dy, da, db):
            cp.wait_send()

    for cp in (zq, zd, dq, dd):
        cp.wait_send()
    dd.wait_recv()

    for zz in range(2):
        same = (zz == z) & (z == y) & (y == x) & (x == c)
        for k, dst in enumerate([w13.at[pl.ds(2 * zz, 2), 0, :, pl.ds(0, 512)],
                                 w13.at[pl.ds(2 * zz, 2), 0, :, pl.ds(512, 512)],
                                 w2.at[pl.ds(2 * zz, 2), 0]]):
            @pl.when(jnp.logical_not(same))
            def _():
                pltpu.make_async_copy(dst, dst, ur.at[zz, k]).wait()
    for same, cp, lc in unit_copies:
        @pl.when(jnp.logical_not(same))
        def _():
            cp.wait_send()

        @pl.when(same)
        def _():
            lc.wait()


def tree_slices(k):
    rows13 = 4096 // CHUNKS
    rows2 = 2048 // CHUNKS
    per13 = 2048 // rows13
    per2 = 512 // rows2
    return [
        (0, (k // per13, 0, pl.ds(pl.multiple_of((k % per13) * rows13, rows13), rows13))),
        (0, (2 + k // per13, 0, pl.ds(pl.multiple_of((k % per13) * rows13, rows13), rows13))),
        (1, (k // per2, 0, pl.ds(pl.multiple_of((k % per2) * rows2, rows2), rows2))),
    ]


def tree_wholes(arrays):
    return [arrays[0].at[pl.ds(0, 2)], arrays[0].at[pl.ds(2, 2)], arrays[1]]


def spread_kernel(root, w13, w2, hot13, hot2, recv, send, csend, crecv):
    rz, ry, rx, rc = root // 8, (root // 4) % 2, (root // 2) % 2, root % 2
    z, y, x, c = coords()
    rel = [x if rx == 0 else 1 - x, y if ry == 0 else 1 - y, z if rz == 0 else 1 - z]
    near = [(z, y, 1 - x, c), (z, 1 - y, x, c), (1 - z, y, x, c)]
    sib = (z, y, x, 1 - c)
    mine = (w13, w2)
    hot = (hot13, hot2)
    relay = c == rc
    at_root = (rel[0] + rel[1] + rel[2]) == 0
    plans = []
    for j in range(3):
        ra, rb, rd = rel[j], rel[(j + 1) % 3], rel[(j + 2) % 3]
        depth = jnp.where(ra == 1, 1 + rb + rd, jnp.where(rb + rd == 0, 0, 2 + rb + rd))
        goes = [
            ((ra + rb + rd) == 0) | ((ra == 1) & ((rb + rd) > 0)),
            (ra == 1) & (rb == 0) & (rd == 0),
            (ra == 1) & (rd == 0),
        ]
        plans.append((depth, goes))

    @pl.when(relay)
    def _():
        def issue(source, j, k, which, index):
            depth, goes = plans[j]
            for step in range(3):
                cp = remote(source[which].at[index], hot[which].at[index],
                            send.at[j, step], recv.at[j, k], near[(j + step) % 3])

                @pl.when(goes[step])
                def _():
                    cp.start()
            remote(source[which].at[index], hot[which].at[index], csend.at[j], crecv.at[j], sib).start()

        @pl.when(at_root)
        def _():
            @pl.loop(0, CHUNKS)
            def _(k):
                for j, (which, index) in enumerate(tree_slices(k)):
                    depth, goes = plans[j]
                    cp = remote(mine[which].at[index], hot[which].at[index],
                                send.at[j, 0], recv.at[j, k], near[j])
                    cp.start()
                for j, (which, index) in enumerate(tree_slices(k)):
                    remote(mine[which].at[index], hot[which].at[index], csend.at[j], crecv.at[j], sib).start()

        @pl.when(jnp.logical_not(at_root))
        def _():
            @pl.loop(1, CHUNKS + 4)
            def _(i):
                for j in range(3):
                    depth, goes = plans[j]
                    k = i - depth

                    @pl.when((k >= 0) & (k < CHUNKS))
                    def _():
                        which, index = tree_slices(k)[j]
                        here = hot[which].at[index]
                        pltpu.make_async_copy(here, here, recv.at[j, k]).wait()
                        issue(hot, j, k, which, index)

        for j, whole in enumerate(tree_wholes(hot)):
            depth, goes = plans[j]
            for step in range(3):
                @pl.when(goes[step])
                def _():
                    pltpu.make_async_copy(whole, whole, send.at[j, step]).wait()
            pltpu.make_async_copy(whole, whole, csend.at[j]).wait()

    @pl.when(jnp.logical_not(relay))
    def _():
        for j, whole in enumerate(tree_wholes(hot)):
            pltpu.make_async_copy(whole, whole, crecv.at[j]).wait()


def pick_kernel(pick, a13, b13, c13, a2, b2, c2, out13, out2):
    for k, (r13, r2) in enumerate(((a13, a2), (b13, b2), (c13, c2))):
        @pl.when(pick[0] == k)
        def _():
            out13[...] = r13[...]
            out2[...] = r2[...]

    @pl.when(pick[0] == 3)
    def _():
        out13[...] = jnp.zeros_like(out13)
        out2[...] = jnp.zeros_like(out2)


def join_kernel(stage, own, other, out):
    layer = pl.program_id(0)

    @pl.when(layer // 2 == stage[0])
    def _():
        out[...] = own[...]

    @pl.when(layer // 2 != stage[0])
    def _():
        out[...] = other[...]


def solution(mesh):
    flat_axes = ('stage', 'expert')
    DMA = pltpu.SemaphoreType.DMA
    side = pltpu.CompilerParams(has_side_effects=True)

    def local_move(w_gate, w_up, w_down, dense, hot_ids, spare_map):
        u13 = jax.ShapeDtypeStruct((4, 1, 2048, 1024), BF16)
        u2 = jax.ShapeDtypeStruct((4, 1, 512, 2048), BF16)
        w13, w2, other = pl.pallas_call(
            move_kernel,
            out_shape=(u13, u2, jax.ShapeDtypeStruct((2, 2048, 2048), BF16)),
            in_specs=[ANY] * 4,
            out_specs=(ANY, ANY, ANY),
            scratch_shapes=[DMA((2, 3)), DMA((2, 3)), DMA((3,)), DMA((12,)), DMA((12,))],
            compiler_params=side,
            name='move',
        )(w_gate, w_up, w_down, dense)

        def spread(root):
            def call(a, b):
                return pl.pallas_call(
                    lambda *refs: spread_kernel(root, *refs),
                    out_shape=(u13, u2),
                    in_specs=[ANY] * 2,
                    out_specs=(ANY, ANY),
                    scratch_shapes=[DMA((3, CHUNKS)), DMA((3, 3)), DMA((3,)), DMA((3,))],
                    compiler_params=side,
                    name='spread%d' % root,
                )(a, b)
            return call

        branches = [spread(root) for root in range(16)]
        a13, a2 = lax.switch(hot_ids[0], branches, w13, w2)
        b13, b2 = lax.switch(hot_ids[1], branches, w13, w2)

        stage = lax.axis_index('stage').astype(jnp.int32)
        rows = 1024
        dense_all = pl.pallas_call(
            join_kernel,
            grid_spec=pltpu.PrefetchScalarGridSpec(
                num_scalar_prefetch=1,
                grid=(4, 2048 // rows),
                in_specs=[
                    pl.BlockSpec((1, rows, 2048), lambda l, i, s: (jnp.where(l // 2 == s[0], l % 2, 1 - s[0]), jnp.where(l // 2 == s[0], i, (1 - s[0]) * (2048 // rows - 1)), 0)),
                    pl.BlockSpec((1, rows, 2048), lambda l, i, s: (jnp.where(l // 2 != s[0], l % 2, s[0]), jnp.where(l // 2 != s[0], i, s[0] * (2048 // rows - 1)), 0)),
                ],
                out_specs=pl.BlockSpec((1, rows, 2048), lambda l, i, s: (l, i, 0)),
            ),
            out_shape=jax.ShapeDtypeStruct((4, 2048, 2048), BF16),
            name='join',
        )(stage.reshape(1), dense, other)

        me = stage * 8 + lax.axis_index('expert').astype(jnp.int32)
        want = spare_map[0]
        home = jnp.where(want == 0, hot_ids[0], hot_ids[1])
        pick = jnp.where(want < 0, 3, jnp.where(home == me, 2, want)).astype(jnp.int32)

        def spec(shape, source):
            def index(l, i, s):
                on = s[0] == source
                return (jnp.where(on, l, 0), 0, jnp.where(on, i, 0), 0)
            return pl.BlockSpec(shape, index)

        s13, s2 = (1, 1, 1024, 1024), (1, 1, 256, 2048)
        spare13, spare2 = pl.pallas_call(
            pick_kernel,
            grid_spec=pltpu.PrefetchScalarGridSpec(
                num_scalar_prefetch=1,
                grid=(4, 2),
                in_specs=[spec(s13, k) for k in range(3)] + [spec(s2, k) for k in range(3)],
                out_specs=[pl.BlockSpec(s13, lambda l, i, s: (l, 0, i, 0)),
                           pl.BlockSpec(s2, lambda l, i, s: (l, 0, i, 0))],
            ),
            out_shape=(u13, u2),
            name='pick',
        )(pick.reshape(1), a13, b13, w13, a2, b2, w2)
        return w13, w2, dense_all, spare13, spare2

    expert_spec = P('stage', 'expert', None, None)
    unit_spec = P(None, flat_axes, None, None)
    return jax.shard_map(
        local_move,
        mesh=mesh,
        in_specs=(expert_spec, expert_spec, expert_spec, P('stage', None, None), P(None), P(flat_axes)),
        out_specs=(unit_spec, unit_spec, P(None, None, None), unit_spec, unit_spec),
        check_vma=False,
    )
```

time: 2250 us -> 792 us (0.35)
  the two profiles are of different devices: /device:TPU:0 before, /device:TPU:10 now
where the time goes in v1:
time: 792 us
  Pallas kernels  764 us (96%)
  local copies, waits for them, and re-layouts  23.7 us (3%)
    pallas_call x1, Pallas kernels, local_move(): pl.pallas_call(move_kernel, out_shape=(u13, u2, jax.ShapeDtypeStruct((2,...  409 us
    pallas_call x2, Pallas kernels, call(): pl.pallas_call(lambda *refs: spread_kernel(root, *refs), out_shape=(u13,...  310 us
    pallas_call x1, Pallas kernels, local_move(): pl.pallas_call(join_kernel, grid_spec=pltpu.PrefetchScalarGridSpec(num_sc...  23.6 us
    unnamed x2, local copies, waits for them, and re-layouts  22.3 us
    pallas_call x1, Pallas kernels, local_move(): pl.pallas_call(pick_kernel, grid_spec=pltpu.PrefetchScalarGridSpec(num_sc...  20.3 us

profile of v1, /device:TPU:10, one launch (start us, length us, event | category | flops | bytes accessed | tf_op | source)
XLA Modules:
  0.0 791.5 jit_solution(10322416087810090573)
XLA Ops:
  0.6 1.3 fusion
  3.9 409.4 %move.1 = (bf16[4,1,2048,1024]{3,2,1,0:T(8,128)(2,1)}, bf16[4,1,512,2048]{3,2,1,0:T(8,128)(2,1)}, bf16[2,2048,2048]{2,1,0:T(8,128)(2,1)}) custom-call(bf16[2,1,2048,1024]{3,2,1,0:T(8,128)(2,1)} %gate.1, bf16[2,1,2048,1024]{3,2,1,0:T(8,128)(2,1)} %up.1, bf16[2,1,1024,2048]{3,2,1,0:T(8,128)(2,1)} %down.1, bf16[2,2048,2048]{2,1,0:T(8,128)(2,1)} %own.1), custom_call_target="tpu_custom_call" | custom-call | tf_op jit(solution)/shard_map/move/pallas_call | solution.py:270
  413.9 138.7 %conditional.2 = ((bf16[4,1,2048,1024]{3,2,1,0:T(8,128)(2,1)}, bf16[4,1,512,2048]{3,2,1,0:T(8,128)(2,1)})) conditional(s32[]{:T(128)} %clamp.6, (bf16[4,1,2048,1024]{3,2,1,0:T(8,128)(2,1)}, bf16[4,1,512,2048]{3,2,1,0:T(8,128)(2,1)}) %tuple.104, (bf16[4,1,2048,1024]{3,2,1,0:T(8,128)(2,1)}, ...), branch_computations={%region_0.0_spmd, %region_1.0_spmd, %region_2.0_spmd, %region_3.0_... | conditional | bytes 8 | solution.py:294
  414.0 138.6 %spread9.2 = (bf16[4,1,2048,1024]{3,2,1,0:T(8,128)(2,1)}, bf16[4,1,512,2048]{3,2,1,0:T(8,128)(2,1)}) custom-call(bf16[4,1,2048,1024]{3,2,1,0:T(8,128)(2,1)} %get-tuple-element.146.refs_0_, bf16[4,1,512,2048]{3,2,1,0:T(8,128)(2,1)} %get-tuple-element.147.refs_1_), custom_call_target="tpu_custom_call" | custom-call | tf_op jit(solution)/shard_map/cond/branch_9_fun/spread9/pallas_call | solution.py:282
  553.3 172.0 %conditional.3 = ((bf16[4,1,2048,1024]{3,2,1,0:T(8,128)(2,1)}, bf16[4,1,512,2048]{3,2,1,0:T(8,128)(2,1)})) conditional(s32[]{:T(128)} %clamp.7, (bf16[4,1,2048,1024]{3,2,1,0:T(8,128)(2,1)}, bf16[4,1,512,2048]{3,2,1,0:T(8,128)(2,1)}) %tuple.104, (bf16[4,1,2048,1024]{3,2,1,0:T(8,128)(2,1)}, ...), branch_computations={%region_16.0_spmd, %region_17.0_spmd, %region_18.0_spmd, %region_1... | conditional | bytes 8 | solution.py:295
  553.3 171.8 %spread0.3 = (bf16[4,1,2048,1024]{3,2,1,0:T(8,128)(2,1)}, bf16[4,1,512,2048]{3,2,1,0:T(8,128)(2,1)}) custom-call(bf16[4,1,2048,1024]{3,2,1,0:T(8,128)(2,1)} %get-tuple-element.160.refs_0_, bf16[4,1,512,2048]{3,2,1,0:T(8,128)(2,1)} %get-tuple-element.161.refs_1_), custom_call_target="tpu_custom_call" | custom-call | tf_op jit(solution)/shard_map/cond/branch_0_fun/spread0/pallas_call | solution.py:282
  725.3 20.3 %pick.1 = (bf16[4,1,2048,1024]{3,2,1,0:T(8,128)(2,1)}, bf16[4,1,512,2048]{3,2,1,0:T(8,128)(2,1)}) custom-call(s32[1]{0:T(128)} %bitcast.4.pick, bf16[4,1,2048,1024]{3,2,1,0:T(8,128)(2,1)} %get-tuple-element.209.a13, bf16[4,1,2048,1024]{3,2,1,0:T(8,128)(2,1)} %get-tuple-element.210.b13, bf16[4,1,2048,1024]{3,2,1,0:T(8,128)(2,1)} %get-tuple-element.286.c13, ...), custom_call_target="tpu_custom_call" | custom-call | tf_op jit(solution)/shard_map/pick/pallas_call | solution.py:326
  745.6 23.6 %join.1 = bf16[4,2048,2048]{2,1,0:T(8,128)(2,1)} custom-call(s32[1]{0:T(128)} %bitcast.stage, bf16[2,2048,2048]{2,1,0:T(8,128)(2,1)} %own.1, bf16[2,2048,2048]{2,1,0:T(8,128)(2,1)} %get-tuple-element.208.other), custom_call_target="tpu_custom_call" | custom-call | tf_op jit(solution)/shard_map/join/pallas_call | solution.py:299
  769.2 13.9 %copy.78 = bf16[4,1,2048,1024]{3,2,1,0:T(8,128)(2,1)} copy(bf16[4,1,2048,1024]{3,2,1,0:T(8,128)(2,1)} %get-tuple-element.286.c13) | data formatting | bytes 33554432
  783.1 8.4 %copy.79 = bf16[4,1,512,2048]{3,2,1,0:T(8,128)(2,1)} copy(bf16[4,1,512,2048]{3,2,1,0:T(8,128)(2,1)} %get-tuple-element.287.c2) | data formatting | bytes 16777216

commit v2 on v0

v2 whole, which is shorter than its diff:
```python
import jax
import jax.numpy as jnp
from jax import lax
from jax.experimental import pallas as pl
from jax.experimental.pallas import tpu as pltpu
from jax.sharding import PartitionSpec as P


MESH = pl.DeviceIdType.MESH
ANY = pl.BlockSpec(memory_space=pl.ANY)
BF16 = jnp.bfloat16
CHUNKS = 16
SLACK = 3
ROWS = 32
DIRECT = 8
QUARTER = 14


def coords():
    s = lax.axis_index('stage')
    g = lax.axis_index('expert')
    return s, g // 4, (g // 2) % 2, g % 2


def remote(src, dst, send_sem, recv_sem, target):
    z, y, x, c = target
    return pltpu.make_async_remote_copy(
        src_ref=src, dst_ref=dst, send_sem=send_sem, recv_sem=recv_sem,
        device_id=(z, y * 4 + x * 2 + c), device_id_type=MESH)


def arrived(ref, sem):
    pltpu.make_async_copy(ref, ref, sem).wait()


def spread_kernel(unit, layer, gate, up, down, dense, hot13, hot2, other,
                  recv, send, qrecv, trecv, qsend):
    expert, piece = unit // 2, unit % 2
    ry, rx, rc = expert // 4, (expert // 2) % 2, expert % 2
    z, y, x, c = coords()
    is_r = c != x
    is_s = c == x
    late = jnp.where(is_s, 1, 0)
    near = [(z, y, 1 - x, c), (z, 1 - y, x, c), (1 - z, y, x, c), (z, y, x, 1 - c)]
    rel_x = x if rx == 0 else 1 - x
    rel_y = y if ry == 0 else 1 - y

    def tree(t):
        h, j = t // 3, t % 3
        rel = [rel_x, rel_y, (z + h) % 2]
        pick = lambda n: jnp.where(n == 0, rel[0], jnp.where(n == 1, rel[1], rel[2]))
        ra, rd = pick(j), pick((j + 2) % 3)
        total = rel[0] + rel[1] + rel[2]
        at_root = total == 0
        origin = at_root & (c == rc)
        first = at_root | ((ra == 1) & (total > 1))
        second = (ra == 1) & (total == 1)
        third = (ra == 1) & (rd == 0)
        goes = []
        for d, who in enumerate((is_s, is_r, is_r)):
            turn = (d + 3 - j) % 3
            goes.append(who & (((turn == 0) & first) | ((turn == 1) & second) | ((turn == 2) & third)))
        goes.append(is_r | at_root)
        depth = jnp.where(ra == 1, total, 2 + total)
        lag = jnp.where(at_root, jnp.where(origin, 0, 1), SLACK * depth + late)
        return h, j, goes, origin, lag

    def hot13_at(h, j, k):
        rows = 4096 // CHUNKS
        l, r = k // (CHUNKS // 2), k % (CHUNKS // 2)
        band = pl.ds(pl.multiple_of(r * rows, rows), rows)
        here = hot13.at[2 * h + l, 0, band, pl.ds(pl.multiple_of(j * 512, 512), 512)]
        return here, (l, 0, band, pl.ds(piece * 512, 512))

    def hot2_at(h, k):
        rows = 1024 // CHUNKS
        l, r = k // (CHUNKS // 2), k % (CHUNKS // 2)
        here = hot2.at[2 * h + l, 0, pl.ds(pl.multiple_of(r * rows, rows), rows), :]
        return here, (l, 0, pl.ds(pl.multiple_of(piece * 512 + r * rows, rows), rows), slice(None))

    def rows_of(s, m):
        q = ((y + s // 2) % 2) * 2 + (x + s % 2) % 2
        return pl.ds(pl.multiple_of((DIRECT + q * QUARTER + m) * ROWS, ROWS), ROWS)

    @pl.loop(0, CHUNKS + 4 * SLACK + 2)
    def _(i):
        @pl.when(is_r & (i < QUARTER))
        def _():
            rows = rows_of(0, i)
            remote(dense.at[layer, rows], other.at[rows], qsend.at[0], qrecv.at[0, i], near[2]).start()

        @pl.when(is_r & (i < DIRECT))
        def _():
            rows = pl.ds(pl.multiple_of(i * ROWS, ROWS), ROWS)
            remote(dense.at[layer, rows], other.at[rows], qsend.at[1], trecv.at[i], near[2]).start()

        @pl.loop(0, 6)
        def _(t):
            h, j, goes, origin, lag = tree(t)
            k = i - lag

            def pass_on(source, here):
                for d in range(4):
                    @pl.when(goes[d])
                    def _():
                        remote(source, here, send.at[t, d], recv.at[t, k], near[d]).start()

            def give(source, here):
                @pl.loop(0, 4)
                def _(d):
                    on = (goes[0] & (d == 0)) | (goes[1] & (d == 1)) | (goes[2] & (d == 2)) | (goes[3] & (d == 3))

                    @pl.when(on)
                    def _():
                        flip = lambda bit, n: jnp.where(d == n, 1 - bit, bit)
                        remote(source, here, send.at[t, d], recv.at[t, k],
                               (flip(z, 2), flip(y, 1), flip(x, 0), flip(c, 3))).start()

            @pl.when((k >= 0) & (k < CHUNKS))
            def _():
                @pl.when(j < 2)
                def _():
                    here, index = hot13_at(h, j, k)
                    for n, source in enumerate((gate, up)):
                        @pl.when(origin & (j == n))
                        def _():
                            give(source.at[index], here)

                    @pl.when(jnp.logical_not(origin))
                    def _():
                        arrived(here, recv.at[t, k])
                        pass_on(here, here)

                @pl.when(j == 2)
                def _():
                    here, index = hot2_at(h, k)

                    @pl.when(origin)
                    def _():
                        give(down.at[index], here)

                    @pl.when(jnp.logical_not(origin))
                    def _():
                        arrived(here, recv.at[t, k])
                        pass_on(here, here)

        @pl.loop(0, 4)
        def _(s):
            m = i - (SLACK + (SLACK + 1) * (s % 2) + SLACK * (s // 2) + late)

            @pl.when((m >= 0) & (m < QUARTER))
            def _():
                rows = rows_of(s, m)
                here = other.at[rows]
                arrived(here, qrecv.at[s, m])

                @pl.when(is_r & ((s == 0) | ((s == 1) & (m % 2 == 0))))
                def _():
                    remote(here, here, qsend.at[2], qrecv.at[s + 2, m], near[1]).start()

                @pl.when(is_s & ((s == 0) | ((s == 2) & (m % 2 == 1))))
                def _():
                    remote(here, here, qsend.at[3], qrecv.at[s + 1, m], near[0]).start()

                @pl.when(is_r)
                def _():
                    remote(here, here, qsend.at[4], qrecv.at[s, m], near[3]).start()

        m = i - (SLACK + late)

        @pl.when((m >= 0) & (m < DIRECT))
        def _():
            here = other.at[pl.ds(pl.multiple_of(m * ROWS, ROWS), ROWS)]
            arrived(here, trecv.at[m])

            @pl.when(is_r)
            def _():
                remote(here, here, qsend.at[5], trecv.at[m], near[3]).start()

    @pl.loop(0, 6)
    def _(t):
        _, _, goes, origin, _ = tree(t)

        @pl.when(origin)
        def _():
            @pl.loop(0, CHUNKS)
            def _(k):
                arrived(hot2_at(0, 0)[0], recv.at[t, k])

        for d in range(4):
            @pl.when(goes[d])
            def _():
                arrived(hot2.at[pl.ds(0, 2)], send.at[t, d])

    quarter, direct = QUARTER * ROWS, DIRECT * ROWS

    @pl.when(is_r)
    def _():
        arrived(other.at[pl.ds(0, quarter)], qsend.at[0])
        arrived(other.at[pl.ds(0, direct)], qsend.at[1])
        arrived(other.at[pl.ds(0, quarter + quarter // 2)], qsend.at[2])
        arrived(other.at[pl.ds(0, 4 * quarter)], qsend.at[4])
        arrived(other.at[pl.ds(0, direct)], qsend.at[5])

    @pl.when(is_s)
    def _():
        arrived(other.at[pl.ds(0, quarter + quarter // 2)], qsend.at[3])


def cut_kernel(stage, gate, up, a13, b13):
    for s, (left, right) in enumerate(((a13, b13), (b13, a13))):
        @pl.when(stage[0] == s)
        def _():
            left[0, :, :512] = gate[0, 0, :, :512]
            left[0, :, 512:] = up[0, 0, :, :512]
            right[0, :, :512] = gate[0, 0, :, 512:]
            right[0, :, 512:] = up[0, 0, :, 512:]


def copy_kernel(pick, *refs):
    *sources, out = refs
    choice = pick[pl.program_id(0)]
    for k, ref in enumerate(sources):
        @pl.when(choice == k)
        def _():
            out[...] = ref[...].reshape(out.shape)

    @pl.when(choice == len(sources))
    def _():
        out[...] = jnp.zeros_like(out)


def pick_layers(picks, where, to, sources, shape, rows, base=None):
    blocks = shape[-2] // rows
    count = picks.shape[0]
    table = jnp.concatenate([picks, where, to]).astype(jnp.int32)

    def spec(k, source):
        lead = (1,) * (len(source.shape) - 2)

        def index(n, i, t):
            on = t[n] == k
            return (jnp.where(on, t[count + n], 0),) + (0,) * (len(lead) - 1) + (jnp.where(on, i, 0), 0)

        return pl.BlockSpec(lead + (rows, shape[-1]), index)

    lead = (1,) * (len(shape) - 2)
    extra = [] if base is None else [base]
    body = copy_kernel if base is None else lambda pick, kept, *refs: copy_kernel(pick, *refs)
    return pl.pallas_call(
        body,
        grid_spec=pltpu.PrefetchScalarGridSpec(
            num_scalar_prefetch=1,
            grid=(count, blocks),
            in_specs=[ANY] * len(extra) + [spec(k, source) for k, source in enumerate(sources)],
            out_specs=pl.BlockSpec(
                lead + (rows, shape[-1]), lambda n, i, t: (t[2 * count + n],) + (0,) * (len(lead) - 1) + (i, 0)),
        ),
        out_shape=jax.ShapeDtypeStruct(shape, BF16),
        input_output_aliases={} if base is None else {1: 0},
        cost_estimate=pl.CostEstimate(flops=0, bytes_accessed=4 * count * shape[-2] * shape[-1], transcendentals=0),
    )(table, *extra, *sources)


def permute_pairs(swap):
    pairs = [(z * 8 + e, 2 * e + (1 - z if swap else z)) for z in range(2) for e in range(8)]
    return [(a, b) for a, b in pairs if a != b]


def solution(mesh):
    flat_axes = ('stage', 'expert')
    DMA = pltpu.SemaphoreType.DMA
    side = pltpu.CompilerParams(has_side_effects=True)
    u13 = jax.ShapeDtypeStruct((4, 1, 2048, 1024), BF16)
    u2 = jax.ShapeDtypeStruct((4, 1, 512, 2048), BF16)

    def spread(unit, layer):
        def call(*args):
            return pl.pallas_call(
                lambda *refs: spread_kernel(unit, layer, *refs),
                out_shape=(u13, u2, jax.ShapeDtypeStruct((2048, 2048), BF16)),
                in_specs=[ANY] * 4,
                out_specs=(ANY, ANY, ANY),
                scratch_shapes=[DMA((6, CHUNKS)), DMA((6, 4)), DMA((4, QUARTER)), DMA((DIRECT,)), DMA((6,))],
                compiler_params=side,
                cost_estimate=pl.CostEstimate(flops=0, bytes_accessed=300 << 20, transcendentals=0),
            )(*args)

        return call

    def local_move(w_gate, w_up, w_down, dense, hot_ids, spare_map):
        stage = lax.axis_index('stage').astype(jnp.int32)
        core = (lax.axis_index('expert') % 2).astype(jnp.int32)
        layers = jnp.arange(4, dtype=jnp.int32)

        def permute(value, swap):
            return lax.ppermute(value, flat_axes, permute_pairs(swap))

        def slice2(piece):
            return pl.pallas_call(
                lambda t, ref, out: copy_kernel(t, ref, out),
                grid_spec=pltpu.PrefetchScalarGridSpec(
                    num_scalar_prefetch=1,
                    grid=(2, 2),
                    in_specs=[pl.BlockSpec((1, 1, 256, 2048), lambda l, i, t: (l, 0, 2 * t[2] + i, 0))],
                    out_specs=pl.BlockSpec((1, 256, 2048), lambda l, i, t: (l, i, 0)),
                ),
                out_shape=jax.ShapeDtypeStruct((2, 512, 2048), BF16),
            )(jnp.stack([0 * piece, 0 * piece, piece]), w_down)

        own2 = slice2(stage)
        own2, later = lax.optimization_barrier((own2, stage))
        a2 = permute(own2, 0)
        far2 = slice2(1 - later)
        b2 = permute(far2, 1)
        rows = 512
        own13, far13 = pl.pallas_call(
            cut_kernel,
            grid_spec=pltpu.PrefetchScalarGridSpec(
                num_scalar_prefetch=1,
                grid=(2, 2048 // rows),
                in_specs=[pl.BlockSpec((1, 1, rows, 1024), lambda l, i, s: (l, 0, i, 0))] * 2,
                out_specs=[pl.BlockSpec((1, rows, 1024), lambda l, i, s: (l, i, 0))] * 2,
            ),
            out_shape=(jax.ShapeDtypeStruct((2, 2048, 1024), BF16),) * 2,
            name='cut',
        )(later.reshape(1), w_gate, w_up)

        def spread_all(unit, h):
            branches = [spread(root, h) for root in range(16)]
            return lax.switch(unit, branches, w_gate, w_up, w_down, dense)

        own13, far13, first, second = lax.optimization_barrier((own13, far13, hot_ids[0], hot_ids[1]))
        h13, h2, o0 = spread_all(first, 0)
        own13, o0, second = lax.optimization_barrier((own13, o0, second))
        a13 = permute(own13, 0)
        g13, g2, o1 = spread_all(second, 1)
        far13, o1 = lax.optimization_barrier((far13, o1))
        b13 = permute(far13, 1)

        dense_all = pick_layers(
            jnp.where(layers // 2 == stage, 0, 1 + layers % 2), jnp.where(layers // 2 == stage, layers % 2, 0), layers,
            (dense, o0.reshape(1, 2048, 2048), o1.reshape(1, 2048, 2048)), (4, 2048, 2048), 1024)
        want = jnp.where(spare_map[0] < 0, 2, spare_map[0]) + 0 * layers
        spare13 = pick_layers(want, layers, layers, (h13, g13), u13.shape, 2048)
        spare2 = pick_layers(want, layers, layers, (h2, g2), u2.shape, 512)

        flat = stage * 8 + lax.axis_index('expert').astype(jnp.int32)
        keeps = jnp.where((flat == 0) | (flat == 15), 1, 0)
        pair = layers[:2]
        w2 = pick_layers(jnp.where(layers // 2 == core, keeps, 2), layers % 2, layers, (a2, own2, b2), u2.shape, 512)
        w13 = pick_layers(keeps + 0 * pair, pair, 2 * core + pair, (a13, own13), u13.shape, 2048)
        w13 = pick_layers(0 * pair, pair, 2 - 2 * core + pair, (b13,), u13.shape, 2048, w13)
        return w13, w2, dense_all, spare13, spare2

    expert_spec = P('stage', 'expert', None, None)
    unit_spec = P(None, flat_axes, None, None)

    return jax.shard_map(
        local_move,
        mesh=mesh,
        in_specs=(expert_spec, expert_spec, expert_spec, P('stage', None, None), P(None), P(flat_axes)),
        out_specs=(unit_spec, unit_spec, P(None, None, None), unit_spec, unit_spec),
        check_vma=False,
    )
```

time: 2250 us -> 606 us (0.27)
  the two profiles are of different devices: /device:TPU:0 before, /device:TPU:5 now
where the time goes in v2:
time: 606 us; the launch traced here: 605 us
  Pallas kernels  468 us (77%)
  waiting for transfers between devices  122 us (20%)
  starting transfers between devices  8.86 us (1%)
    pallas_call x2, Pallas kernels, call(): pl.pallas_call(lambda *refs: spread_kernel(unit, layer, *refs), out_shape...  372 us
    ppermute x4, waiting for transfers between devices, permute(): return lax.ppermute(value, flat_axes, permute_pairs(swap))  122 us
    pallas_call x6, Pallas kernels, pick_layers(): pl.pallas_call(body, grid_spec=pltpu.PrefetchScalarGridSpec(num_scalar_pr...  71.1 us
    pallas_call x1, Pallas kernels, local_move(): pl.pallas_call(cut_kernel, grid_spec=pltpu.PrefetchScalarGridSpec(num_sca...  13.6 us
  transfers between devices with their start and end apart: 4, of which 2 were waited for; matrix products, arithmetic and copies ran while one was open for 0% of the time, Pallas kernels for 50%

profile of v2, /device:TPU:5, one launch (start us, length us, event | category | flops | bytes accessed | tf_op | source)
XLA Modules:
  0.0 605.3 jit_solution(14159327526009741242)
XLA Ops:
  0.6 0.6 stack.13.t
  1.2 5.4 shard_map.101.refs_1_
  6.7 0.6 fusion
  7.2 13.6 %cut.1 = (bf16[2,2048,1024]{2,1,0:T(8,128)(2,1)}, bf16[2,2048,1024]{2,1,0:T(8,128)(2,1)}) custom-call(s32[1]{0:T(128)} %bitcast.1.stage, bf16[2,1,2048,1024]{3,2,1,0:T(8,128)(2,1)} %gate.1, bf16[2,1,2048,1024]{3,2,1,0:T(8,128)(2,1)} %up.1), custom_call_target="tpu_custom_call" | custom-call | tf_op jit(solution)/shard_map/cut/pallas_call | solution.py:317
  21.5 141.8 %conditional.2 = ((bf16[4,1,2048,1024]{3,2,1,0:T(8,128)(2,1)}, bf16[4,1,512,2048]{3,2,1,0:T(8,128)(2,1)}, bf16[2048,2048]{1,0:T(8,128)(2,1)})) conditional(s32[]{:T(128)} %clamp.6, (bf16[2,1,2048,1024]{3,2,1,0:T(8,128)(2,1)}, bf16[2,1,2048,1024]{3,2,1,0:T(8,128)(2,1)}, bf16[2,1,1024,2048]{3,2,1,0:T(8,128)(2,1)}, ...), branch_computations={%region_0.1_spmd, %region_1.2_spmd, %region_2.3_spmd, %region_3.4_... | conditional | bytes 314572800 | solution.py:331
  21.6 141.5 %branch_5_fun.2 = (bf16[4,1,2048,1024]{3,2,1,0:T(8,128)(2,1)}, bf16[4,1,512,2048]{3,2,1,0:T(8,128)(2,1)}, bf16[2048,2048]{1,0:T(8,128)(2,1)}) custom-call(bf16[2,1,2048,1024]{3,2,1,0:T(8,128)(2,1)} %get-tuple-element.276.refs_0_, bf16[2,1,2048,1024]{3,2,1,0:T(8,128)(2,1)} %get-tuple-element.277.refs_1_, ...), custom_call_target="tpu_custom_call" | custom-call | bytes 314572800 | tf_op jit(solution)/shard_map/cond/branch_5_fun/pallas_call | solution.py:279
  163.3 1.9 collective-permute-start
  165.9 230.8 %conditional.3 = ((bf16[4,1,2048,1024]{3,2,1,0:T(8,128)(2,1)}, bf16[4,1,512,2048]{3,2,1,0:T(8,128)(2,1)}, bf16[2048,2048]{1,0:T(8,128)(2,1)})) conditional(s32[]{:T(128)} %clamp.7, (bf16[2,1,2048,1024]{3,2,1,0:T(8,128)(2,1)}, bf16[2,1,2048,1024]{3,2,1,0:T(8,128)(2,1)}, bf16[2,1,1024,2048]{3,2,1,0:T(8,128)(2,1)}, ...), branch_computations={%region_16.17_spmd, %region_17.18_spmd, %region_18.19_spmd, %regio... | conditional | bytes 314572800 | solution.py:331
  165.9 230.5 %branch_15_fun.3 = (bf16[4,1,2048,1024]{3,2,1,0:T(8,128)(2,1)}, bf16[4,1,512,2048]{3,2,1,0:T(8,128)(2,1)}, bf16[2048,2048]{1,0:T(8,128)(2,1)}) custom-call(bf16[2,1,2048,1024]{3,2,1,0:T(8,128)(2,1)} %get-tuple-element.380.refs_0_, bf16[2,1,2048,1024]{3,2,1,0:T(8,128)(2,1)} %get-tuple-element.381.refs_1_, ...), custom_call_target="tpu_custom_call" | custom-call | bytes 314572800 | tf_op jit(solution)/shard_map/cond/branch_15_fun/pallas_call | solution.py:279
  396.7 0.1 collective-permute-start.1
  396.8 0.6 stack.15.t
  397.4 5.4 shard_map.104
  402.8 6.9 %collective-permute-start.2 = (bf16[2,512,2048]{2,1,0:T(8,128)(2,1)}, bf16[2,512,2048]{2,1,0:T(8,128)(2,1)}, u32[]{:S(2)}, u32[]{:S(2)}) collective-permute-start(bf16[2,512,2048]{2,1,0:T(8,128)(2,1)} %shard_map.101.refs_1_), channel_id=1, source_target_pairs={{1,2},{2,4},{3,6},{4,8},{5,10},{6,12},{7,14},{8,1},{9,3},{10,5},{1... | collective-permute-start | bytes 12582920 | tf_op jit(solution)/shard_map/ppermute | solution.py:297
  410.4 0.6 add_add_fusion.2.pick
  410.9 13.4 %shard_map.107 = bf16[4,1,2048,1024]{3,2,1,0:T(8,128)(2,1)} custom-call(s32[12]{0:T(128)} %add_add_fusion.2.pick, bf16[4,1,2048,1024]{3,2,1,0:T(8,128)(2,1)} %get-tuple-element.423.refs_0_, bf16[4,1,2048,1024]{3,2,1,0:T(8,128)(2,1)} %get-tuple-element.424.refs_1_), custom_call_target="tpu_custom_call" | custom-call | bytes 33554432 | tf_op jit(solution)/shard_map/pallas_call | solution.py:250
  424.4 8.4 %shard_map.108 = bf16[4,1,512,2048]{3,2,1,0:T(8,128)(2,1)} custom-call(s32[12]{0:T(128)} %add_add_fusion.2.pick, bf16[4,1,512,2048]{3,2,1,0:T(8,128)(2,1)} %get-tuple-element.425.refs_0_, bf16[4,1,512,2048]{3,2,1,0:T(8,128)(2,1)} %get-tuple-element.426.refs_1_), custom_call_target="tpu_custom_call" | custom-call | bytes 16777216 | tf_op jit(solution)/shard_map/pallas_call | solution.py:250
  432.8 0.7 add_add_fusion.1
  433.5 25.8 %shard_map.106 = bf16[4,2048,2048]{2,1,0:T(8,128)(2,1)} custom-call(s32[12]{0:T(128)} %get-tuple-element.427.pick, bf16[2,2048,2048]{2,1,0:T(8,128)(2,1)} %refs_0_.1, bf16[1,2048,2048]{2,1,0:T(8,128)(2,1)} %bitcast.10, bf16[1,2048,2048]{2,1,0:T(8,128)(2,1)} %bitcast.11), custom_call_target="tpu_custom_call" | custom-call | bytes 67108864 | tf_op jit(solution)/shard_map/pallas_call | solution.py:250
  459.3 0.6 pad_add_fusion.1
  459.9 76.2 %collective-permute-done.3.refs_2_ = bf16[2,512,2048]{2,1,0:T(8,128)(2,1)} collective-permute-done((bf16[2,512,2048]{2,1,0:T(8,128)(2,1)}, bf16[2,512,2048]{2,1,0:T(8,128)(2,1)}, u32[]{:S(2)}, u32[]{:S(2)}) %collective-permute-start.3) | collective-permute-done | bytes 4194336 | tf_op jit(solution)/shard_map/ppermute | solution.py:297
  536.1 45.8 %collective-permute-done.2.refs_0_ = bf16[2,512,2048]{2,1,0:T(8,128)(2,1)} collective-permute-done((bf16[2,512,2048]{2,1,0:T(8,128)(2,1)}, bf16[2,512,2048]{2,1,0:T(8,128)(2,1)}, u32[]{:S(2)}, u32[]{:S(2)}) %collective-permute-start.2) | collective-permute-done | bytes 4194336 | tf_op jit(solution)/shard_map/ppermute | solution.py:297
  581.9 9.1 %shard_map.105 = bf16[4,1,512,2048]{3,2,1,0:T(8,128)(2,1)} custom-call(s32[12]{0:T(128)} %get-tuple-element.428.pick, bf16[2,512,2048]{2,1,0:T(8,128)(2,1)} %collective-permute-done.2.refs_0_, bf16[2,512,2048]{2,1,0:T(8,128)(2,1)} %shard_map.101.refs_1_, bf16[2,512,2048]{2,1,0:T(8,128)(2,1)} %collective-permute-done.3.refs_2_), custom_call_target="tpu_custom_call" | custom-call | bytes 16777216 | tf_op jit(solution)/shard_map/pallas_call | solution.py:250
  591.0 7.8 %shard_map.102.kept = bf16[4,1,2048,1024]{3,2,1,0:T(8,128)(2,1)} custom-call(s32[6]{0:T(128)} %get-tuple-element.431.pick, bf16[2,2048,1024]{2,1,0:T(8,128)(2,1)} %collective-permute-done.refs_0_, bf16[2,2048,1024]{2,1,0:T(8,128)(2,1)} %get-tuple-element.415.refs_1_), custom_call_target="tpu_custom_call" | custom-call | bytes 16777216 | tf_op jit(solution)/shard_map/pallas_call | solution.py:250
  598.8 6.5 %shard_map.103 = bf16[4,1,2048,1024]{3,2,1,0:T(8,128)(2,1)} custom-call(s32[6]{0:T(128)} %get-tuple-element.432.pick, bf16[4,1,2048,1024]{3,2,1,0:T(8,128)(2,1)} %shard_map.102.kept, bf16[2,2048,1024]{2,1,0:T(8,128)(2,1)} %collective-permute-done.1.refs_0_), custom_call_target="tpu_custom_call", output_to_operand_aliasing={{}: (1, {})} | custom-call | bytes 16777216 | tf_op jit(solution)/shard_map/pallas_call | solution.py:250
  (14 shorter events, 0.0 us)
Async XLA Ops:
  0.6 6.0 copy-start
  163.3 427.7 %collective-permute-start = (bf16[2,2048,1024]{2,1,0:T(8,128)(2,1)}, bf16[2,2048,1024]{2,1,0:T(8,128)(2,1)}, u32[]{:S(2)}, u32[]{:S(2)}) collective-permute-start(bf16[2,2048,1024]{2,1,0:T(8,128)(2,1)} %get-tuple-element.415.refs_1_), channel_id=1, source_target_pairs={{1,2},{2,4},{3,6},{4,8},{5,10},{6,12},{7,14},{8,1},{9,3},{10,5},{1... | collective-permute-start | bytes 25165832 | tf_op jit(solution)/shard_map/ppermute | solution.py:297
  396.7 202.1 %collective-permute-start.1 = (bf16[2,2048,1024]{2,1,0:T(8,128)(2,1)}, bf16[2,2048,1024]{2,1,0:T(8,128)(2,1)}, u32[]{:S(2)}, u32[]{:S(2)}) collective-permute-start(bf16[2,2048,1024]{2,1,0:T(8,128)(2,1)} %get-tuple-element.419), channel_id=1, source_target_pairs={{0,1},{1,3},{2,5},{3,7},{4,9},{5,11},{6,13},{7,15},{8,0},{9,2},{10... | collective-permute-start | bytes 25165832 | tf_op jit(solution)/shard_map/ppermute | solution.py:297
  402.8 133.3 %collective-permute-start.3 = (bf16[2,512,2048]{2,1,0:T(8,128)(2,1)}, bf16[2,512,2048]{2,1,0:T(8,128)(2,1)}, u32[]{:S(2)}, u32[]{:S(2)}) collective-permute-start(bf16[2,512,2048]{2,1,0:T(8,128)(2,1)} %shard_map.104), channel_id=1, source_target_pairs={{0,1},{1,3},{2,5},{3,7},{4,9},{5,11},{6,13},{7,15},{8,0},{9,2},{10... | collective-permute-start | bytes 12582920 | tf_op jit(solution)/shard_map/ppermute | solution.py:297
  402.8 179.1 %collective-permute-start.2 = (bf16[2,512,2048]{2,1,0:T(8,128)(2,1)}, bf16[2,512,2048]{2,1,0:T(8,128)(2,1)}, u32[]{:S(2)}, u32[]{:S(2)}) collective-permute-start(bf16[2,512,2048]{2,1,0:T(8,128)(2,1)} %shard_map.101.refs_1_), channel_id=1, source_target_pairs={{1,2},{2,4},{3,6},{4,8},{5,10},{6,12},{7,14},{8,1},{9,3},{10,5},{1... | collective-permute-start | bytes 12582920 | tf_op jit(solution)/shard_map/ppermute | solution.py:297

commit v3 on v2

--- a/solution.py
+++ b/solution.py
@@ -33,8 +33,11 @@
     pltpu.make_async_copy(ref, ref, sem).wait()
 
 
-def spread_kernel(unit, layer, gate, up, down, dense, hot13, hot2, other,
-                  recv, send, qrecv, trecv, qsend):
+def spread_kernel(unit, layer, gate, up, down, dense, hot13, hot2, other, *rest):
+    if layer == 0:
+        own13, far_a, far_b, recv, send, qrecv, trecv, qsend, local, cut = rest
+    else:
+        recv, send, qrecv, trecv, qsend = rest
     expert, piece = unit // 2, unit % 2
     ry, rx, rc = expert // 4, (expert // 2) % 2, expert % 2
     z, y, x, c = coords()
@@ -82,8 +85,30 @@
         q = ((y + s // 2) % 2) * 2 + (x + s % 2) % 2
         return pl.ds(pl.multiple_of((DIRECT + q * QUARTER + m) * ROWS, ROWS), ROWS)
 
+    def load(side, n):
+        columns = pl.ds(pl.multiple_of(((z + side) % 2) * 512, 512), 512)
+        return pltpu.make_async_copy((gate, up)[n].at[:, 0, :, columns], cut.at[side, :, :, pl.ds(n * 512, 512)], local.at[side, n])
+
+    def store(n):
+        src = cut.at[0] if n == 0 else cut.at[1, n - 1]
+        return pltpu.make_async_copy(src, (own13, far_a, far_b)[n], local.at[2, n])
+
+    if layer == 0:
+        for side in range(2):
+            for n in range(2):
+                load(side, n).start()
+
     @pl.loop(0, CHUNKS + 4 * SLACK + 2)
     def _(i):
+        if layer == 0:
+            @pl.when(i == SLACK)
+            def _():
+                for side in range(2):
+                    for n in range(2):
+                        load(side, n).wait()
+                for n in range(3):
+                    store(n).start()
+
         @pl.when(is_r & (i < QUARTER))
         def _():
             rows = rows_of(0, i)
@@ -192,29 +217,23 @@
             def _():
                 arrived(hot2.at[pl.ds(0, 2)], send.at[t, d])
 
+    if layer == 0:
+        for n in range(3):
+            store(n).wait()
+
     quarter, direct = QUARTER * ROWS, DIRECT * ROWS
 
     @pl.when(is_r)
     def _():
         arrived(other.at[pl.ds(0, quarter)], qsend.at[0])
         arrived(other.at[pl.ds(0, direct)], qsend.at[1])
-        arrived(other.at[pl.ds(0, quarter + quarter // 2)], qsend.at[2])
+        arrived(other.at[pl.ds(0, (QUARTER + (QUARTER + 1) // 2) * ROWS)], qsend.at[2])
         arrived(other.at[pl.ds(0, 4 * quarter)], qsend.at[4])
         arrived(other.at[pl.ds(0, direct)], qsend.at[5])
 
     @pl.when(is_s)
     def _():
-        arrived(other.at[pl.ds(0, quarter + quarter // 2)], qsend.at[3])
-
-
-def cut_kernel(stage, gate, up, a13, b13):
-    for s, (left, right) in enumerate(((a13, b13), (b13, a13))):
-        @pl.when(stage[0] == s)
-        def _():
-            left[0, :, :512] = gate[0, 0, :, :512]
-            left[0, :, 512:] = up[0, 0, :, :512]
-            right[0, :, :512] = gate[0, 0, :, 512:]
-            right[0, :, 512:] = up[0, 0, :, 512:]
+        arrived(other.at[pl.ds(0, (QUARTER + QUARTER // 2) * ROWS)], qsend.at[3])
 
 
 def copy_kernel(pick, *refs):
@@ -275,13 +294,19 @@
     u2 = jax.ShapeDtypeStruct((4, 1, 512, 2048), BF16)
 
     def spread(unit, layer):
+        out_shape = (u13, u2, jax.ShapeDtypeStruct((2048, 2048), BF16))
+        buffers = []
+        if layer == 0:
+            out_shape += (jax.ShapeDtypeStruct((2, 2048, 1024), BF16),) + (jax.ShapeDtypeStruct((2048, 1024), BF16),) * 2
+            buffers = [DMA((3, 3)), pltpu.VMEM((2, 2, 2048, 1024), BF16)]
+
         def call(*args):
             return pl.pallas_call(
                 lambda *refs: spread_kernel(unit, layer, *refs),
-                out_shape=(u13, u2, jax.ShapeDtypeStruct((2048, 2048), BF16)),
+                out_shape=out_shape,
                 in_specs=[ANY] * 4,
-                out_specs=(ANY, ANY, ANY),
-                scratch_shapes=[DMA((6, CHUNKS)), DMA((6, 4)), DMA((4, QUARTER)), DMA((DIRECT,)), DMA((6,))],
+                out_specs=(ANY,) * len(out_shape),
+                scratch_shapes=[DMA((6, CHUNKS)), DMA((6, 4)), DMA((4, QUARTER)), DMA((DIRECT,)), DMA((6,))] + buffers,
                 compiler_params=side,
                 cost_estimate=pl.CostEstimate(flops=0, bytes_accessed=300 << 20, transcendentals=0),
             )(*args)
@@ -312,31 +337,20 @@
         own2, later = lax.optimization_barrier((own2, stage))
         a2 = permute(own2, 0)
         far2 = slice2(1 - later)
-        b2 = permute(far2, 1)
-        rows = 512
-        own13, far13 = pl.pallas_call(
-            cut_kernel,
-            grid_spec=pltpu.PrefetchScalarGridSpec(
-                num_scalar_prefetch=1,
-                grid=(2, 2048 // rows),
-                in_specs=[pl.BlockSpec((1, 1, rows, 1024), lambda l, i, s: (l, 0, i, 0))] * 2,
-                out_specs=[pl.BlockSpec((1, rows, 1024), lambda l, i, s: (l, i, 0))] * 2,
-            ),
-            out_shape=(jax.ShapeDtypeStruct((2, 2048, 1024), BF16),) * 2,
-            name='cut',
-        )(later.reshape(1), w_gate, w_up)
 
         def spread_all(unit, h):
             branches = [spread(root, h) for root in range(16)]
             return lax.switch(unit, branches, w_gate, w_up, w_down, dense)
 
-        own13, far13, first, second = lax.optimization_barrier((own13, far13, hot_ids[0], hot_ids[1]))
-        h13, h2, o0 = spread_all(first, 0)
-        own13, o0, second = lax.optimization_barrier((own13, o0, second))
+        far2, first = lax.optimization_barrier((far2, hot_ids[0]))
+        b2 = permute(far2, 1)
+        h13, h2, o0, own13, far_a, far_b = spread_all(first, 0)
+        second, o0 = lax.optimization_barrier((hot_ids[1], o0))
         a13 = permute(own13, 0)
         g13, g2, o1 = spread_all(second, 1)
-        far13, o1 = lax.optimization_barrier((far13, o1))
-        b13 = permute(far13, 1)
+        far_a, far_b, o1 = lax.optimization_barrier((far_a, far_b, o1))
+        far_a = permute(far_a, 1)
+        far_b = permute(far_b, 1)
 
         dense_all = pick_layers(
             jnp.where(layers // 2 == stage, 0, 1 + layers % 2), jnp.where(layers // 2 == stage, layers % 2, 0), layers,
@@ -347,10 +361,12 @@
 
         flat = stage * 8 + lax.axis_index('expert').astype(jnp.int32)
         keeps = jnp.where((flat == 0) | (flat == 15), 1, 0)
-        pair = layers[:2]
+        pair, zero = layers[:2], 0 * layers
         w2 = pick_layers(jnp.where(layers // 2 == core, keeps, 2), layers % 2, layers, (a2, own2, b2), u2.shape, 512)
         w13 = pick_layers(keeps + 0 * pair, pair, 2 * core + pair, (a13, own13), u13.shape, 2048)
-        w13 = pick_layers(0 * pair, pair, 2 - 2 * core + pair, (b13,), u13.shape, 2048, w13)
+        for n, far in enumerate((far_a, far_b)):
+            w13 = pick_layers(zero[:1], zero[:1], (2 - 2 * core + n).reshape(1), (far.reshape(1, 2048, 1024),),
+                              u13.shape, 1024, w13)
         return w13, w2, dense_all, spare13, spare2
 
     expert_spec = P('stage', 'expert', None, None)

time: 606 us -> 580 us (0.957)
  the two profiles are of different devices: /device:TPU:5 before, /device:TPU:0 now
where the time goes in v3:
time: 580 us; the launch traced here: 579 us
  Pallas kernels  537 us (93%)
  waiting for transfers between devices  23.1 us (4%)
  starting transfers between devices  10.6 us (2%)
    pallas_call x2, Pallas kernels, call(): pl.pallas_call(lambda *refs: spread_kernel(unit, layer, *refs), out_shape...  458 us
    pallas_call x7, Pallas kernels, pick_layers(): pl.pallas_call(body, grid_spec=pltpu.PrefetchScalarGridSpec(num_scalar_pr...  68.4 us
    ppermute x5, waiting for transfers between devices, permute(): return lax.ppermute(value, flat_axes, permute_pairs(swap))  23.1 us
  transfers between devices with their start and end apart: 5, of which 1 were waited for; matrix products, arithmetic and copies ran while one was open for 1% of the time, Pallas kernels for 65%

profile of v3, /device:TPU:0, one launch (start us, length us, event | category | flops | bytes accessed | tf_op | source)
XLA Modules:
  0.0 578.8 jit_solution(2868127647441341337)
XLA Ops:
  0.6 0.6 stack.13.t
  1.2 5.4 shard_map.101.refs_1_
  6.6 0.6 stack.15.t
  7.2 5.4 shard_map.102
  12.6 0.6 fusion
  13.9 143.9 %conditional.2 = ((bf16[4,1,2048,1024]{3,2,1,0:T(8,128)(2,1)}, bf16[4,1,512,2048]{3,2,1,0:T(8,128)(2,1)}, bf16[2048,2048]{1,0:T(8,128)(2,1)}, bf16[2,2048,1024]{...) conditional(s32[]{:T(128)} %clamp.6, ...), branch_computations={%region_0.1_spmd, %region_1.2_spmd, %region_2.3_spmd, %region_3.4_... | conditional | bytes 314572800 | solution.py:343
  13.9 143.7 %branch_5_fun.2 = (bf16[4,1,2048,1024]{3,2,1,0:T(8,128)(2,1)}, bf16[4,1,512,2048]{3,2,1,0:T(8,128)(2,1)}, bf16[2048,2048]{1,0:T(8,128)(2,1)}, bf16[2,2048,1024]{...) custom-call(bf16[2,1,2048,1024]{3,2,1,0:T(8,128)(2,1)} %get-tuple-element.276.refs_0_, ...), custom_call_target="tpu_custom_call" | custom-call | bytes 314572800 | tf_op jit(solution)/shard_map/cond/branch_5_fun/pallas_call | solution.py:304
  157.8 3.9 collective-permute-start
  161.7 2.6 collective-permute-start.3
  165.0 314.5 %conditional.3 = ((bf16[4,1,2048,1024]{3,2,1,0:T(8,128)(2,1)}, bf16[4,1,512,2048]{3,2,1,0:T(8,128)(2,1)}, bf16[2048,2048]{1,0:T(8,128)(2,1)})) conditional(s32[]{:T(128)} %clamp.7, (bf16[2,1,2048,1024]{3,2,1,0:T(8,128)(2,1)}, bf16[2,1,2048,1024]{3,2,1,0:T(8,128)(2,1)}, bf16[2,1,1024,2048]{3,2,1,0:T(8,128)(2,1)}, ...), branch_computations={%region_16.17_spmd, %region_17.18_spmd, %region_18.19_spmd, %regio... | conditional | bytes 314572800 | solution.py:343
  165.1 314.2 %branch_15_fun.3 = (bf16[4,1,2048,1024]{3,2,1,0:T(8,128)(2,1)}, bf16[4,1,512,2048]{3,2,1,0:T(8,128)(2,1)}, bf16[2048,2048]{1,0:T(8,128)(2,1)}) custom-call(bf16[2,1,2048,1024]{3,2,1,0:T(8,128)(2,1)} %get-tuple-element.380.refs_0_, bf16[2,1,2048,1024]{3,2,1,0:T(8,128)(2,1)} %get-tuple-element.381.refs_1_, ...), custom_call_target="tpu_custom_call" | custom-call | bytes 314572800 | tf_op jit(solution)/shard_map/cond/branch_15_fun/pallas_call | solution.py:304
  479.6 4.1 collective-permute-start.2
  483.6 0.6 concatenate.20.pick
  484.2 0.6 concatenate.19.pick
  486.1 10.3 %shard_map.108 = bf16[4,1,2048,1024]{3,2,1,0:T(8,128)(2,1)} custom-call(s32[12]{0:T(128)} %add_add_fusion.2.pick, bf16[4,1,2048,1024]{3,2,1,0:T(8,128)(2,1)} %get-tuple-element.421.refs_0_, bf16[4,1,2048,1024]{3,2,1,0:T(8,128)(2,1)} %get-tuple-element.422.refs_1_), custom_call_target="tpu_custom_call" | custom-call | bytes 33554432 | tf_op jit(solution)/shard_map/pallas_call | solution.py:269
  496.4 6.5 %shard_map.109 = bf16[4,1,512,2048]{3,2,1,0:T(8,128)(2,1)} custom-call(s32[12]{0:T(128)} %add_add_fusion.2.pick, bf16[4,1,512,2048]{3,2,1,0:T(8,128)(2,1)} %get-tuple-element.423.refs_0_, bf16[4,1,512,2048]{3,2,1,0:T(8,128)(2,1)} %get-tuple-element.424.refs_1_), custom_call_target="tpu_custom_call" | custom-call | bytes 16777216 | tf_op jit(solution)/shard_map/pallas_call | solution.py:269
  503.0 0.6 add_add_fusion.1
  503.6 25.8 %shard_map.107 = bf16[4,2048,2048]{2,1,0:T(8,128)(2,1)} custom-call(s32[12]{0:T(128)} %get-tuple-element.425.pick, bf16[2,2048,2048]{2,1,0:T(8,128)(2,1)} %refs_0_.1, bf16[1,2048,2048]{2,1,0:T(8,128)(2,1)} %bitcast.13, bf16[1,2048,2048]{2,1,0:T(8,128)(2,1)} %bitcast.14), custom_call_target="tpu_custom_call" | custom-call | bytes 67108864 | tf_op jit(solution)/shard_map/pallas_call | solution.py:269
  529.4 0.6 pad_add_fusion.pick
  530.0 9.1 %shard_map.106 = bf16[4,1,512,2048]{3,2,1,0:T(8,128)(2,1)} custom-call(s32[12]{0:T(128)} %get-tuple-element.426.pick, bf16[2,512,2048]{2,1,0:T(8,128)(2,1)} %collective-permute-done.3.refs_0_, bf16[2,512,2048]{2,1,0:T(8,128)(2,1)} %shard_map.101.refs_1_, bf16[2,512,2048]{2,1,0:T(8,128)(2,1)} %collective-permute-done.4.refs_2_), custom_call_target="tpu_custom_call" | custom-call | bytes 16777216 | tf_op jit(solution)/shard_map/pallas_call | solution.py:269
  539.1 7.8 %shard_map.103.kept = bf16[4,1,2048,1024]{3,2,1,0:T(8,128)(2,1)} custom-call(s32[6]{0:T(128)} %pad_add_fusion.pick, bf16[2,2048,1024]{2,1,0:T(8,128)(2,1)} %collective-permute-done.refs_0_, bf16[2,2048,1024]{2,1,0:T(8,128)(2,1)} %get-tuple-element.409.refs_1_), custom_call_target="tpu_custom_call" | custom-call | bytes 16777216 | tf_op jit(solution)/shard_map/pallas_call | solution.py:269
  546.9 4.4 shard_map.104.kept
  551.3 23.1 %collective-permute-done.2 = bf16[2048,1024]{1,0:T(8,128)(2,1)} collective-permute-done((bf16[2048,1024]{1,0:T(8,128)(2,1)}, bf16[2048,1024]{1,0:T(8,128)(2,1)}, u32[]{:S(2)}, u32[]{:S(2)}) %collective-permute-start.2) | collective-permute-done | bytes 4194336 | tf_op jit(solution)/shard_map/ppermute | solution.py:322
  574.4 4.4 shard_map.105
  (18 shorter events, 0.7 us)
Async XLA Ops:
  6.6 6.0 %copy-start = (s32[2]{0:T(128)S(1)}, s32[2]{0:T(128)}, u32[]{:S(2)}) copy-start(s32[2]{0:T(128)} %param.42) | copy-start | bytes 28
  157.8 381.2 %collective-permute-start = (bf16[2,2048,1024]{2,1,0:T(8,128)(2,1)}, bf16[2,2048,1024]{2,1,0:T(8,128)(2,1)}, u32[]{:S(2)}, u32[]{:S(2)}) collective-permute-start(bf16[2,2048,1024]{2,1,0:T(8,128)(2,1)} %get-tuple-element.409.refs_1_), channel_id=1, source_target_pairs={{1,2},{2,4},{3,6},{4,8},{5,10},{6,12},{7,14},{8,1},{9,3},{10,5},{1... | collective-permute-start | bytes 25165832 | tf_op jit(solution)/shard_map/ppermute | solution.py:322
  161.7 368.3 %collective-permute-start.4 = (bf16[2,512,2048]{2,1,0:T(8,128)(2,1)}, bf16[2,512,2048]{2,1,0:T(8,128)(2,1)}, u32[]{:S(2)}, u32[]{:S(2)}) collective-permute-start(bf16[2,512,2048]{2,1,0:T(8,128)(2,1)} %shard_map.102), channel_id=1, source_target_pairs={{0,1},{1,3},{2,5},{3,7},{4,9},{5,11},{6,13},{7,15},{8,0},{9,2},{10... | collective-permute-start | bytes 12582920 | tf_op jit(solution)/shard_map/ppermute | solution.py:322
  161.7 368.3 %collective-permute-start.3 = (bf16[2,512,2048]{2,1,0:T(8,128)(2,1)}, bf16[2,512,2048]{2,1,0:T(8,128)(2,1)}, u32[]{:S(2)}, u32[]{:S(2)}) collective-permute-start(bf16[2,512,2048]{2,1,0:T(8,128)(2,1)} %shard_map.101.refs_1_), channel_id=1, source_target_pairs={{1,2},{2,4},{3,6},{4,8},{5,10},{6,12},{7,14},{8,1},{9,3},{10,5},{1... | collective-permute-start | bytes 12582920 | tf_op jit(solution)/shard_map/ppermute | solution.py:322
  479.5 67.4 %collective-permute-start.1 = (bf16[2048,1024]{1,0:T(8,128)(2,1)}, bf16[2048,1024]{1,0:T(8,128)(2,1)}, u32[]{:S(2)}, u32[]{:S(2)}) collective-permute-start(bf16[2048,1024]{1,0:T(8,128)(2,1)} %get-tuple-element.415), channel_id=1, source_target_pairs={{0,1},{1,3},{2,5},{3,7},{4,9},{5,11},{6,13},{7,15},{8,0},{9,2},{10... | collective-permute-start | bytes 12582920 | tf_op jit(solution)/shard_map/ppermute | solution.py:322
  479.6 94.8 %collective-permute-start.2 = (bf16[2048,1024]{1,0:T(8,128)(2,1)}, bf16[2048,1024]{1,0:T(8,128)(2,1)}, u32[]{:S(2)}, u32[]{:S(2)}) collective-permute-start(bf16[2048,1024]{1,0:T(8,128)(2,1)} %get-tuple-element.416), channel_id=1, source_target_pairs={{0,1},{1,3},{2,5},{3,7},{4,9},{5,11},{6,13},{7,15},{8,0},{9,2},{10... | collective-permute-start | bytes 12582920 | tf_op jit(solution)/shard_map/ppermute | solution.py:322
